TPU v7x, 128 devices: a whole 4x4x4 slice. The times are simulated.
128 devices in a mesh: expert: 16 (over y, x), mp: 8 (over z, core).
Axes of the slice: x: 4, y: 4, z: 4, core: 2. Of those that a mesh axis runs over, the one named last changes fastest.
Arguments:
- tokens: bfloat16 [2048, 7168], P('expert', 'mp'), may hold values from -0.625 to 0.625
- cotangent: bfloat16 [2048, 8, 2048], P('expert', None, 'mp'), may hold values from -3 to 3
- weights: bfloat16 [32, 7168, 2048], P('expert', 'mp'), may hold values from -0.0625 to 0.0625
- steps: float32 [32, 2048], P('expert', 'mp'), may hold values from 0.002 to 0.02
- expert_ids: int32 [2048, 8], P('expert'), may hold values from 0 to 31, all different within a row; in each aligned block of 128 rows (0 to 127, 128 to 255, ...) at most 64 rows name the same one
Outputs:
- token_grads: bfloat16 [2048, 7168], P('expert', 'mp')
- weight_grads: bfloat16 [32, 7168, 2048], P('expert', 'mp')
- step_grads: float32 [32, 2048], P('expert', 'mp')
Inputs may be any that keep to these rules, and one draw needn't show every extreme that they name: `expert_ids`: each row names 8 different experts; among the 128 rows of one index of the expert axis, no expert is named by more than 64 rows, a bound that some block reaches of them.
All inputs are finite; a program needn't handle non-finite values.
Results may differ from a plain program's by a relative error of at most 0.0058.
Values may be sent and summed in bfloat16 or wider, within the bound.
A program may use at most 128 MiB of HBM per device.

v0:
```python
import math

import jax
import jax.numpy as jnp
from jax import lax
from jax.sharding import PartitionSpec as P

qmax = 7.0
wiggle = 0.9
two_pi = 6.283185307179586


def quantize(weight_f, step_f):
    scaled = weight_f / step_f
    squash = jnp.tanh(scaled / qmax)
    clipped = qmax * squash
    angles = two_pi * clipped
    stair = clipped - wiggle * jnp.sin(angles) / two_pi
    slopes = (1.0 - wiggle * jnp.cos(angles)) * (1.0 - squash * squash)
    return (step_f * stair, slopes, stair - scaled * slopes)


def slot_table(routes_flat, experts, capacity):
    one_hot = (routes_flat[:, None] == jnp.arange(experts, dtype=jnp.int32)[None, :]).astype(
        jnp.int32
    )
    before = jnp.cumsum(one_hot, axis=0) - one_hot
    position = jnp.sum(before * one_hot, axis=1)
    slot_of = routes_flat * capacity + position
    route_count = routes_flat.shape[0]
    source_of = jnp.full((experts * capacity,), route_count, jnp.int32)
    source_of = source_of.at[slot_of].set(jnp.arange(route_count, dtype=jnp.int32))
    return (slot_of, source_of)


def per_device(tokens, cotangent, weights, steps, expert_ids):
    groups = lax.axis_size("expert")
    local_experts = weights.shape[0]
    experts = groups * local_experts
    tok_rows, top_k = expert_ids.shape
    capacity = tok_rows // 2
    width_part = tokens.shape[1]
    slot_of, source_of = slot_table(expert_ids.reshape(-1), experts, capacity)
    token_of = source_of // top_k
    padded_x = jnp.concatenate([tokens, jnp.zeros((1, width_part), tokens.dtype)], axis=0)
    x_slots = padded_x[token_of].reshape(groups, local_experts, capacity, width_part)
    full_steps = lax.all_gather(steps, "mp", axis=1, tiled=True)
    levels, slopes, step_slopes = quantize(weights.astype(jnp.float32), full_steps[:, None, :])
    quantized = levels.astype(jnp.bfloat16)
    part_width = cotangent.shape[2]
    padded_g = jnp.concatenate(
        [
            cotangent.reshape(tok_rows * top_k, part_width),
            jnp.zeros((1, part_width), cotangent.dtype),
        ],
        axis=0,
    )
    g_slots = padded_g[source_of].reshape(groups, local_experts, capacity, part_width)
    x_recv, g_part = (
        lax.all_to_all(x_slots, "expert", split_axis=0, concat_axis=0, tiled=True),
        lax.all_to_all(g_slots, "expert", split_axis=0, concat_axis=0, tiled=True),
    )
    g_recv = lax.all_gather(g_part, "mp", axis=3, tiled=True)
    raw = jnp.einsum("sjcd,sjcf->jdf", x_recv, g_recv, preferred_element_type=jnp.float32)
    weight_out = (raw * slopes).astype(jnp.bfloat16)
    full_width = width_part * lax.axis_size("mp")
    partial_steps = jnp.sum(raw * step_slopes, axis=1)
    step_out = lax.psum_scatter(partial_steps, "mp", scatter_dimension=1, tiled=True) * (
        1.0 / math.sqrt(full_width * qmax)
    )
    back_slots = jnp.einsum(
        "sjcf,jdf->sjcd", g_recv, quantized, preferred_element_type=jnp.float32
    ).astype(jnp.bfloat16)
    returned = lax.all_to_all(back_slots, "expert", split_axis=0, concat_axis=0, tiled=True)
    per_route = returned.reshape(experts * capacity, width_part)[slot_of]
    token_out = (
        per_route.reshape(tok_rows, top_k, width_part)
        .astype(jnp.float32)
        .sum(axis=1)
        .astype(jnp.bfloat16)
    )
    return (token_out, weight_out, step_out)


def solution(mesh):
    return jax.shard_map(
        per_device,
        mesh=mesh,
        in_specs=(
            P("expert", "mp"),
            P("expert", None, "mp"),
            P("expert", "mp", None),
            P("expert", "mp"),
            P("expert", None),
        ),
        out_specs=(P("expert", "mp"), P("expert", "mp", None), P("expert", "mp")),
        check_vma=False,
    )
```

profile of v0, /device:TPU:1, one launch (start us, length us, event | category | flops | bytes accessed | tf_op | source)
XLA Modules:
  0.0 304.6 jit_solution(9049717152482495890)
XLA Ops:
  7.2 0.8 copy.17
  8.2 0.7 broadcast_multiply_fusion
  8.9 9.0 %reduce-window.6 = s32[32,8,128]{2,1,0:T(8,128)S(1)} reduce-window(s32[32,8,128]{2,1,0:T(8,128)S(1)} %fusion.17, s32[]{:T(128)} %constant.43.clone.1), window={size=1x1x128 pad=0_0x0_0x127_0}, to_apply=%region_0.0 | reduce-window | flops 4161536 | bytes 262148 | tf_op jit(solution)/shard_map/reduce-window
  18.0 0.1 copy.19
  18.6 4.3 %scatter_custom_fusion = s32[2048]{0:T(1024)S(1)} fusion(s32[1024]{0:T(1024)S(1)} %bitcast.58, s32[1024]{0:T(1024)S(1)} %iota.11, s32[]{:T(128)} %constant.41.clone.1), kind=kCustom, calls=%fused_computation.44 | custom fusion | bytes 8196 | tf_op jit(solution)/shard_map/scatter | solution.py:32
  23.0 1.1 concatenate.6
  24.1 7.5 %gather_fusion = bf16[2048,256]{1,0:T(8,128)(2,1)S(1)} fusion(bf16[1025,256]{1,0:T(8,128)(2,1)S(1)} %concatenate.6, s32[2048]{0:T(1024)S(1)} %get-tuple-element.6), kind=kCustom, calls=%fused_computation | custom fusion | bytes 2105344 | tf_op jit(solution)/shard_map/gather | solution.py:58
  31.6 23.4 %all_to_all.15 = bf16[16,2,64,256]{3,2,1,0:T(8,128)(2,1)S(1)} all-to-all(bf16[16,2,64,256]{3,2,1,0:T(8,128)(2,1)S(1)} %bitcast.52), channel_id=1, replica_groups=mesh['expert'=16,'mp'=8] {'expert'}, dimensions={0} | all-to-all | bytes 2097152 | tf_op jit(solution)/shard_map/all_to_all | solution.py:61
  55.0 1.1 copy.21
  56.2 9.5 %gather_fusion.2 = bf16[2048,896]{1,0:T(8,128)(2,1)} fusion(bf16[129,896]{1,0:T(8,128)(2,1)S(1)} %concatenate.7, s32[2048]{0:T(1024)S(1)} %get-tuple-element.5), kind=kCustom, calls=%fused_computation.2 | custom fusion | bytes 7348224 | tf_op jit(solution)/shard_map/gather | solution.py:46
  65.7 4.6 %all-to-all-start.2 = ((bf16[16,2,64,896]{3,2,1,0:T(8,128)(2,1)}), bf16[16,2,64,896]{3,2,1,0:T(8,128)(2,1)}, u32[]{:S(2)}, u32[]{:S(2)}) async-start(bf16[16,2,64,896]{3,2,1,0:T(8,128)(2,1)} %bitcast.50), calls=%async_computation.2 | async-start | bytes 7340032 | tf_op jit(solution)/shard_map/all_to_all | solution.py:60
  70.2 14.9 %all_gather.6 = f32[2,2048]{1,0:T(2,128)S(1)} all-gather(f32[2,256]{1,0:T(2,128)S(1)} %copy-done.1), channel_id=1, replica_groups=mesh['expert'=16,'mp'=8] {'mp'}, dimensions={1}, use_global_device_ids=true | all-gather | bytes 18432 | tf_op jit(solution)/shard_map/all_gather | solution.py:47
  85.2 25.1 %all-gather.2.cloned.1.call-done = bf16[16,2,64,2048]{3,2,0,1:T(8,128)(2,1)} async-done(((bf16[16,2,64,256]{3,2,0,1:T(8,128)(2,1)}), bf16[16,2,64,2048]{3,2,0,1:T(8,128)(2,1)}) %all-gather.2.cloned.1.call-update) | async-done | bytes 8388624 | tf_op jit(solution)/shard_map/all_gather | solution.py:63
  110.2 64.9 %convert_bitcast_fusion = bf16[16,2,64,896]{3,2,0,1:T(8,128)(2,1)S(1)} fusion(bf16[16,2,64,2048]{3,2,0,1:T(8,128)(2,1)} %all-gather.2.cloned.1.call-done, f32[2,2048]{1,0:T(2,128)S(1)} %all_gather.6, bf16[2,896,2048]{2,1,0:T(8,128)(2,1)} %param.7), kind=kOutput, calls=%fused_computation.22 | convolution fusion | flops 7551057920 | bytes 19415040 | tf_op jit(solution)/shard_map/sjcf,jdf->sjcd/dot_general | solution.py:71
  175.2 2.2 copy.22
  177.4 6.6 %all-to-all-start.1 = ((bf16[16,2,64,896]{3,2,1,0:T(8,128)(2,1)}), bf16[16,2,64,896]{3,2,1,0:T(8,128)(2,1)}, u32[]{:S(2)}, u32[]{:S(2)}) async-start(bf16[16,2,64,896]{3,2,1,0:T(8,128)(2,1)} %copy.22), calls=%async_computation.1 | async-start | bytes 7340032 | tf_op jit(solution)/shard_map/all_to_all | solution.py:74
  184.0 0.2 reduce-scatter.4.cloned.1.call-start
  184.2 70.7 %fusion.1 = (f32[2,2048]{1,0:T(2,128)S(1)}, bf16[2,896,2048]{2,1,0:T(8,128)(2,1)}) fusion(f32[2,2048]{1,0:T(2,128)S(1)} %all_gather.6, bf16[2,896,2048]{2,1,0:T(8,128)(2,1)} %param.7, bf16[16,2,64,896]{3,2,1,0:T(8,128)(2,1)} %all-to-all-done.2, bf16[16,2,64,2048]{3,2,0,1:T(8,128)(2,1)} %all-gather.2.cloned.1.call-done), kind=kOutput, calls=%fused_computation.7 | convolution fusion | flops 7582248960 | bytes 26771456 | tf_op jit(solution)/shard_map/sjcd,sjcf->jdf/dot_general | solution.py:64
  254.9 1.4 copy.27
  256.3 30.8 %reduce-scatter.4.cloned.1.call-done = f32[256,2]{1,0:T(8,128)} async-done(((f32[2048,2]{1,0:T(8,128)}), f32[256,2]{1,0:T(8,128)}) %reduce-scatter.4.cloned.1.call-update) | async-done | bytes 2064
  287.1 1.0 copy.28
  288.1 0.6 broadcast_multiply_fusion.1
  288.7 7.2 %gather_fusion.1 = bf16[1024,896]{1,0:T(8,128)(2,1)S(1)} fusion(bf16[2048,896]{1,0:T(8,128)(2,1)} %bitcast.9, s32[1024]{0:T(1024)S(1)} %broadcast_clamp_fusion), kind=kCustom, calls=%fused_computation.1 | custom fusion | bytes 3674112 | tf_op jit(solution)/shard_map/gather | solution.py:75
  295.9 1.9 bitcast_reduce_fusion
  (25 shorter events, 0.9 us)
Async XLA Ops:
  7.2 103.1 %all-gather.2.cloned.1.call-start = ((), (), s32[]{:S(2)}) async-start(), calls=%async_computation.4 | async-start | bytes 9437184 | tf_op jit(solution)/shard_map/all_gather | solution.py:63
  17.9 38.2 %copy-start = (bf16[128,896]{1,0:T(8,128)(2,1)S(1)}, bf16[128,896]{1,0:T(8,128)(2,1)}, u32[]{:S(2)}) copy-start(bf16[128,896]{1,0:T(8,128)(2,1)} %param.5) | copy-start | bytes 688132
  56.2 14.0 %copy-start.1 = (f32[2,256]{1,0:T(2,128)S(1)}, f32[2,256]{1,0:T(2,128)}, u32[]{:S(2)}) copy-start(f32[2,256]{1,0:T(2,128)} %param.8) | copy-start | bytes 6148
  65.7 111.7 %all-to-all-start.2 = ((bf16[16,2,64,896]{3,2,1,0:T(8,128)(2,1)}), bf16[16,2,64,896]{3,2,1,0:T(8,128)(2,1)}, u32[]{:S(2)}, u32[]{:S(2)}) async-start(bf16[16,2,64,896]{3,2,1,0:T(8,128)(2,1)} %bitcast.50), calls=%async_computation.2 | async-start | bytes 7340032 | tf_op jit(solution)/shard_map/all_to_all | solution.py:60
  177.4 111.3 %all-to-all-start.1 = ((bf16[16,2,64,896]{3,2,1,0:T(8,128)(2,1)}), bf16[16,2,64,896]{3,2,1,0:T(8,128)(2,1)}, u32[]{:S(2)}, u32[]{:S(2)}) async-start(bf16[16,2,64,896]{3,2,1,0:T(8,128)(2,1)} %copy.22), calls=%async_computation.1 | async-start | bytes 7340032 | tf_op jit(solution)/shard_map/all_to_all | solution.py:74
  184.0 103.1 %reduce-scatter.4.cloned.1.call-start = ((), (), s32[]{:S(2)}) async-start(), calls=%async_computation.5 | async-start | bytes 1179648
Sparse Core Ops, SparseCore 0:
  56.3 53.9 all-gather.1
  256.4 30.6 reduce-scatter.3
where the time goes:
time: 307 us; the launch traced here: 305 us
  matrix products  136 us (44%)
  waiting for transfers between devices  55.9 us (18%)
  blocking collectives  38.3 us (12%)
  local copies, waits for them, and re-layouts  36.7 us (12%)
  between operations  14.2 us (5%)
  other arithmetic  12.4 us (4%)
  starting transfers between devices  11.4 us (4%)
    dot_general x1, matrix products, per_device(): jnp.einsum('sjcd,sjcf->jdf', x_recv, g_recv, preferred_element_type=jnp.f...  70.7 us
    dot_general x1, matrix products, per_device(): jnp.einsum('sjcf,jdf->sjcd', g_recv, quantized, preferred_element_type=jn...  64.9 us
    unnamed x3, waiting for transfers between devices  30.8 us
    all_gather x1, waiting for transfers between devices, per_device(): g_recv = lax.all_gather(g_part, 'mp', axis=3, tiled=True)  25.1 us
    all_to_all x1, blocking collectives, per_device(): lax.all_to_all(g_slots, 'expert', split_axis=0, concat_axis=0, tiled=True)  23.4 us
    all_gather x1, blocking collectives, per_device(): full_steps = lax.all_gather(steps, 'mp', axis=1, tiled=True)  14.9 us
    gather x1, local copies, waits for them, and re-layouts, per_device(): padded_x[token_of].reshape(groups, local_experts, capacity, width_part)  9.47 us
    another operation x3, other arithmetic  9.15 us
  transfers between devices with their start and end apart: 4, of which 2 were waited for; matrix products, arithmetic and copies ran while one was open for 49% of the time, Pallas kernels for 0%

commit v1 on v0

v1 whole, which is shorter than its diff:
```python
import functools
import math

import jax
import jax.numpy as jnp
from jax import lax
from jax.experimental import pallas as pl
from jax.experimental.pallas import tpu as pltpu
from jax.sharding import PartitionSpec as P

qmax = 7.0
wiggle = 0.9
two_pi = 6.283185307179586
F32 = jnp.float32
BF16 = jnp.bfloat16

SIN = (3.141592640130707, -5.167710083507862, 2.550077523214134, -0.5982912856178576, 0.0776576603009221)
COS = (0.9999999532476082, -4.93479283061961, 4.058411352862034, -1.3318765680776314, 0.2196896110917421)


def poly(z, coefs):
    total = coefs[-1] * z + coefs[-2]
    for coef in coefs[-3::-1]:
        total = total * z + coef
    return total


def quantize(w, step, inv7):
    t = w * inv7
    u = jnp.tanh(t)
    c = qmax * u
    r = c - jnp.floor(c + 0.5)
    z = r * r
    sine = r * poly(z, SIN)
    cosine = poly(z, COS)
    stair = c - (2.0 * wiggle / two_pi) * (sine * cosine)
    slopes = ((1.0 - wiggle) + (2.0 * wiggle) * (sine * sine)) * (1.0 - u * u)
    return step * stair, slopes, stair - (qmax * t) * slopes


def dot(a, b, ca, cb):
    return lax.dot_general(a, b, (((ca,), (cb,)), ((), ())), preferred_element_type=F32)


def upper(n):
    rows = lax.broadcasted_iota(jnp.int32, (n, n), 0)
    cols = lax.broadcasted_iota(jnp.int32, (n, n), 1)
    return jnp.where(rows < cols, 1.0, 0.0).astype(BF16)


def pack_kernel(cap, experts, ids_ref, cot_ref, out_ref):
    chunks = ids_ref.shape[0]
    ahead = upper(128)
    expert = lax.broadcasted_iota(jnp.int32, (experts, 128), 0)
    base = expert.astype(F32) * float(cap)
    seen = jnp.zeros((experts, 1), F32)
    slots = []
    for c in range(chunks):
        hot = jnp.where(expert == ids_ref[c : c + 1, :], 1.0, 0.0)
        place = dot(hot.astype(BF16), ahead, 1, 0) + seen + base
        slots.append(jnp.sum(hot * place, axis=0, keepdims=True))
        seen = seen + jnp.sum(hot, axis=1, keepdims=True)
    slot_row = jnp.concatenate(slots, axis=1).astype(jnp.int32)
    rows = lax.broadcasted_iota(jnp.int32, (128, chunks * 128), 0)
    for j in range(experts * cap // 128):
        pick = jnp.where(rows + 128 * j == slot_row, 1.0, 0.0).astype(BF16)
        out_ref[pl.ds(128 * j, 128), :] = dot(pick, cot_ref[...], 1, 0).astype(BF16)


def pack(ids_rows, cot, cap, experts):
    return pl.pallas_call(
        functools.partial(pack_kernel, cap, experts),
        out_shape=jax.ShapeDtypeStruct((experts * cap, cot.shape[1]), BF16),
        name="pack",
    )(ids_rows, cot)


def quant_kernel(w_ref, s_ref, q_ref, a_ref, b_ref):
    rows, width = w_ref.shape[1:]
    step_rows, step_cols = 16, 512
    for col in range(0, width, step_cols):
        cols = pl.ds(col, step_cols)
        s = s_ref[0, :, cols]
        inv7 = 1.0 / (qmax * s)

        def body(k, carry):
            at = pl.ds(pl.multiple_of(k * step_rows, step_rows), step_rows)
            w = w_ref[0, at, cols].astype(F32)
            q, slopes, step_slopes = quantize(w, s, inv7)
            q_ref[0, at, cols] = q.astype(BF16)
            a_ref[0, at, cols] = slopes.astype(BF16)
            b_ref[0, at, cols] = step_slopes.astype(BF16)
            return carry

        lax.fori_loop(0, rows // step_rows, body, 0, unroll=2)


def quant(weights, steps):
    e, d, f = weights.shape
    tile = 128
    block = pl.BlockSpec((1, tile, f), lambda i, j: (i, j, 0))
    return pl.pallas_call(
        quant_kernel,
        grid=(e, d // tile),
        in_specs=[block, pl.BlockSpec((1, 1, f), lambda i, j: (i, 0, 0))],
        out_specs=[block] * 3,
        out_shape=[jax.ShapeDtypeStruct((e, d, f), BF16)] * 3,
        cost_estimate=pl.CostEstimate(flops=50 * e * d * f, bytes_accessed=8 * e * d * f, transcendentals=e * d * f),
        name="quant",
    )(weights, steps)


def selection(ids_ref, first, local, cap):
    groups, _, toks = ids_ref.shape
    ahead = upper(toks)
    picks = []
    for e in range(local):
        named = [jnp.max(jnp.where(ids_ref[i] == first + e, 1.0, 0.0), axis=0, keepdims=True) for i in range(groups)]
        named = jnp.concatenate(named, axis=0)
        place = dot(named.astype(BF16), ahead, 1, 0)
        picks.append(jnp.where(named > 0.0, place, -1.0).astype(jnp.int32))
    return picks


def pick_of(places, i, cap):
    slot = lax.broadcasted_iota(jnp.int32, (cap, places.shape[1]), 0)
    return jnp.where(slot == places[i : i + 1, :], 1.0, 0.0).astype(BF16)


def back_kernel(cap, ids_ref, g_ref, q_ref, out_ref, sums, backs):
    e = pl.program_id(0)
    local = pl.num_programs(0)
    groups = ids_ref.shape[0]
    g = g_ref[...].reshape(groups * cap, g_ref.shape[-1])
    backs[...] = dot(g, q_ref[0], 1, 1).astype(BF16)
    places = selection(ids_ref, lax.axis_index("expert") * local + e, 1, cap)[0]
    for i in range(groups):
        part = dot(pick_of(places, i, cap), backs[pl.ds(i * cap, cap), :], 0, 0)

        @pl.when(e == 0)
        def _():
            sums[i] = part

        @pl.when(e > 0)
        def _():
            out_ref[i] = (sums[i] + part).astype(BF16)


def back(ids, g, q):
    groups, local, cap, f = g.shape
    d = q.shape[1]
    toks = ids.shape[2]
    return pl.pallas_call(
        functools.partial(back_kernel, cap),
        grid=(local,),
        in_specs=[
            pl.BlockSpec(ids.shape, lambda e: (0, 0, 0)),
            pl.BlockSpec((groups, 1, cap, f), lambda e: (0, e, 0, 0)),
            pl.BlockSpec((1, d, f), lambda e: (e, 0, 0)),
        ],
        out_specs=pl.BlockSpec((groups, toks, d), lambda e: (0, 0, 0)),
        out_shape=jax.ShapeDtypeStruct((groups, toks, d), BF16),
        scratch_shapes=[pltpu.VMEM((groups, toks, d), F32), pltpu.VMEM((groups * cap, d), BF16)],
        cost_estimate=pl.CostEstimate(flops=2 * groups * local * cap * f * d, bytes_accessed=20 << 20, transcendentals=0),
        name="back",
    )(ids, g, q)


def raw_kernel(cap, ids_ref, x_ref, g_ref, a_ref, b_ref, w_ref, s_ref, picked):
    e = pl.program_id(0)
    local = pl.num_programs(0)
    groups = ids_ref.shape[0]

    @pl.when(pl.program_id(1) == 0)
    def _():
        places = selection(ids_ref, lax.axis_index("expert") * local + e, 1, cap)[0]
        for i in range(groups):
            part = dot(pick_of(places, i, cap), x_ref[i], 1, 0).astype(BF16)
            picked[:, pl.ds(i * cap, cap)] = part.T

    g = g_ref[...].reshape(groups * cap, g_ref.shape[-1])
    raw = dot(picked[...], g, 1, 0)
    w_ref[0] = (raw * a_ref[0].astype(F32)).astype(BF16)
    s_ref[0] = jnp.sum(raw * b_ref[0].astype(F32), axis=0, keepdims=True)


def raw_grads(ids, x, g, slopes, step_slopes):
    groups, local, cap, f = g.shape
    d = slopes.shape[1]
    tile = 256
    block = pl.BlockSpec((1, d, tile), lambda e, j: (e, 0, j))
    return pl.pallas_call(
        functools.partial(raw_kernel, cap),
        grid=(local, f // tile),
        in_specs=[
            pl.BlockSpec(ids.shape, lambda e, j: (0, 0, 0)),
            pl.BlockSpec(x.shape, lambda e, j: (0, 0, 0)),
            pl.BlockSpec((groups, 1, cap, tile), lambda e, j: (0, e, 0, j)),
            block,
            block,
        ],
        out_specs=[block, pl.BlockSpec((1, 1, tile), lambda e, j: (e, 0, j))],
        out_shape=[jax.ShapeDtypeStruct((local, d, f), BF16), jax.ShapeDtypeStruct((local, 1, f), F32)],
        scratch_shapes=[pltpu.VMEM((d, groups * cap), BF16)],
        cost_estimate=pl.CostEstimate(flops=2 * groups * local * cap * f * d, bytes_accessed=40 << 20, transcendentals=0),
        name="raw",
    )(ids, x, g, slopes, step_slopes)


def per_device(tokens, cotangent, weights, steps, expert_ids):
    groups = lax.axis_size("expert")
    parts = lax.axis_size("mp")
    local = weights.shape[0]
    experts = groups * local
    toks, top_k = expert_ids.shape
    cap = toks // 2
    width = tokens.shape[1]
    part_f = cotangent.shape[2]
    packed = pack(expert_ids.reshape(-1, 128), cotangent.reshape(toks * top_k, part_f), cap, experts)
    ids = lax.all_gather(expert_ids.T, "expert", axis=0)
    x = lax.all_gather(tokens, "expert", axis=0)
    full_steps = lax.all_gather(steps, "mp", axis=1, tiled=True).reshape(local, 1, -1)
    g_part = lax.all_to_all(packed.reshape(groups, local, cap, part_f), "expert", split_axis=0, concat_axis=0, tiled=True)
    g = lax.all_gather(g_part, "mp", axis=3, tiled=True)
    q, slopes, step_slopes = quant(weights, full_steps)
    backs = back(ids, g, q)
    returned = lax.all_to_all(backs, "expert", split_axis=0, concat_axis=0, tiled=True)
    weight_out, partial_steps = raw_grads(ids, x, g, slopes, step_slopes)
    token_out = returned.astype(F32).sum(axis=0).astype(BF16)
    shares = partial_steps.reshape(local, parts, part_f).transpose(1, 0, 2)
    shares = lax.all_to_all(shares, "mp", split_axis=0, concat_axis=0, tiled=True)
    step_out = shares.sum(axis=0) * (1.0 / math.sqrt(width * parts * qmax))
    return (token_out, weight_out, step_out)


def solution(mesh):
    return jax.shard_map(
        per_device,
        mesh=mesh,
        in_specs=(
            P("expert", "mp"),
            P("expert", None, "mp"),
            P("expert", "mp", None),
            P("expert", "mp"),
            P("expert", None),
        ),
        out_specs=(P("expert", "mp"), P("expert", "mp", None), P("expert", "mp")),
        check_vma=False,
    )
```

time: 307 us -> 251 us (0.82)
  matrix products: 136 us -> 0 us
  Pallas kernels: 0 us -> 75.5 us
  local copies, waits for them, and re-layouts: 36.7 us -> 2.09 us
  waiting for transfers between devices: 55.9 us -> 81.1 us
  blocking collectives: 38.3 us -> 61 us
  other arithmetic: 12.4 us -> 5.26 us
    dot_general x2 -> x0, matrix products: 136 us -> none  [the longest x1 70.7 us: per_device(): jnp.einsum('sjcd,sjcf->jdf', x_recv, g_recv, preferred_element_type=jnp.f...]
    pallas_call x0 -> x4, Pallas kernels: none -> 75.5 us  [the longest x1 25 us: raw_grads(): pl.pallas_call(functools.partial(raw_kernel, cap), grid=(local, f // tile...]
    all_to_all x2, waiting for transfers between devices: 0.01 us -> 55.4 us  [the longest x1 55.4 us: per_device(): lax.all_to_all(backs, 'expert', split_axis=0, concat_axis=0, tiled=True)]
    unnamed x3 -> x2, waiting for transfers between devices: 30.8 us -> 0.7 us
    gather x3 -> x0, local copies, waits for them, and re-layouts: 24.1 us -> none  [the longest x1 9.47 us: per_device(): padded_x[token_of].reshape(groups, local_experts, capacity, width_part)]
    all_gather x1 -> x2, blocking collectives: 14.9 us -> 34.2 us  [the longest x1 18.8 us: per_device(): ids = lax.all_gather(expert_ids.T, 'expert', axis=0)]
    another operation x3 -> x0, other arithmetic: 9.15 us -> none
    scatter x1 -> x0, local copies, waits for them, and re-layouts: 4.32 us -> none  [slot_table(): source_of.at[slot_of].set(jnp.arange(route_count, dtype=jnp.int32))]
  transfers between devices with their start and end apart: 4 -> 4, of which waited for: 2 -> 2; matrix products, arithmetic and copies ran while one was open for 49% -> 1% of each run, Pallas kernels for 0% -> 20%
where the time goes in v1:
time: 251 us; the launch traced here: 250 us
  waiting for transfers between devices  81.1 us (32%)
  Pallas kernels  75.5 us (30%)
  blocking collectives  61 us (24%)
  between operations  14.1 us (6%)
  starting transfers between devices  10.9 us (4%)
  other arithmetic  5.26 us (2%)
    all_to_all x1, waiting for transfers between devices, per_device(): lax.all_to_all(backs, 'expert', split_axis=0, concat_axis=0, tiled=True)  55.4 us
    all_to_all x1, blocking collectives, per_device(): lax.all_to_all(packed.reshape(groups, local, cap, part_f), 'expert', spli...  26.8 us
    pallas_call x1, Pallas kernels, raw_grads(): pl.pallas_call(functools.partial(raw_kernel, cap), grid=(local, f // tile...  25 us
    all_gather x1, waiting for transfers between devices, per_device(): g = lax.all_gather(g_part, 'mp', axis=3, tiled=True)  25 us
    pallas_call x1, Pallas kernels, quant(): pl.pallas_call(quant_kernel, grid=(e, d // tile), in_specs=[block, pl.Blo...  24.1 us
    pallas_call x1, Pallas kernels, back(): pl.pallas_call(functools.partial(back_kernel, cap), grid=(local,), in_spe...  23 us
    all_gather x1, blocking collectives, per_device(): ids = lax.all_gather(expert_ids.T, 'expert', axis=0)  18.8 us
    all_gather x1, blocking collectives, per_device(): lax.all_gather(steps, 'mp', axis=1, tiled=True).reshape(local, 1, -1)  15.4 us
  transfers between devices with their start and end apart: 4, of which 2 were waited for; matrix products, arithmetic and copies ran while one was open for 1% of the time, Pallas kernels for 20%

profile of v1, /device:TPU:1, one launch (start us, length us, event | category | flops | bytes accessed | tf_op | source)
XLA Modules:
  0.0 249.9 jit_solution(12860806853052880577)
XLA Ops:
  7.2 0.0 all-gather.7.cloned.1.call-start
  7.2 0.7 all-gather.7.cloned.1.call-update
  7.9 0.0 all-gather.5.cloned.1.call-start
  7.9 0.8 copy.10
  8.7 0.7 reshape.21.ids_ref
  9.4 3.4 %pack.1 = bf16[2048,256]{1,0:T(8,128)(2,1)} custom-call(s32[8,128]{1,0:T(8,128)} %reshape.21.ids_ref, bf16[1024,256]{1,0:T(8,128)(2,1)} %bitcast.9), custom_call_target="tpu_custom_call" | custom-call | tf_op jit(solution)/shard_map/pack/pallas_call | solution.py:71
  12.8 26.8 %all_to_all.15 = bf16[16,2,64,256]{3,2,1,0:T(8,128)(2,1)} all-to-all(bf16[16,2,64,256]{3,2,1,0:T(8,128)(2,1)} %bitcast.8), channel_id=1, replica_groups=mesh['expert'=16,'mp'=8] {'expert'}, dimensions={0} | all-to-all | bytes 2097152 | tf_op jit(solution)/shard_map/all_to_all | solution.py:223
  39.6 0.0 all-gather.5.cloned.1.call-update
  39.7 15.4 %all_gather.21 = f32[2,2048]{1,0:T(2,128)S(1)} all-gather(f32[2,256]{1,0:T(2,128)} %param.8), channel_id=1, replica_groups=mesh['expert'=16,'mp'=8] {'mp'}, dimensions={1}, use_global_device_ids=true | all-gather | bytes 18432 | tf_op jit(solution)/shard_map/all_gather | solution.py:222
  55.1 0.6 reshape.24.s_ref
  55.7 18.8 %all-gather = s32[128,128]{1,0:T(8,128)} all-gather(s32[8,128]{1,0:T(8,128)} %bitcast.12), channel_id=2, replica_groups=mesh['expert'=16,'mp'=8] {'expert'}, dimensions={0}, use_global_device_ids=true | all-gather | bytes 69632 | tf_op jit(solution)/shard_map/all_gather | solution.py:220
  74.4 24.1 %quant.1 = (bf16[2,896,2048]{2,1,0:T(8,128)(2,1)}, bf16[2,896,2048]{2,1,0:T(8,128)(2,1)}, bf16[2,896,2048]{2,1,0:T(8,128)(2,1)}) custom-call(bf16[2,896,2048]{2,1,0:T(8,128)(2,1)} %w_ref.1, f32[2,1,2048]{2,1,0:T(1,128)} %reshape.24.s_ref), custom_call_target="tpu_custom_call" | custom-call | flops 183500800 | bytes 29360128 | tf_op jit(solution)/shard_map/quant/pallas_call | solution.py:102
  98.6 0.0 all-gather.7.cloned.1.call-done
  98.6 25.0 %all-gather.5.cloned.1.call-done.g_ref = bf16[16,2,64,2048]{3,2,1,0:T(8,128)(2,1)} async-done(((bf16[16,2,64,256]{3,2,1,0:T(8,128)(2,1)}), bf16[16,2,64,2048]{3,2,1,0:T(8,128)(2,1)}) %all-gather.5.cloned.1.call-update) | async-done | bytes 8388624 | tf_op jit(solution)/shard_map/all_gather | solution.py:224
  123.5 25.0 %raw.1 = (bf16[2,896,2048]{2,1,0:T(8,128)(2,1)}, f32[2,1,2048]{2,1,0:T(1,128)}) custom-call(s32[16,8,128]{2,1,0:T(8,128)} %bitcast.10, bf16[16,128,896]{2,1,0:T(8,128)(2,1)} %bitcast.13, bf16[16,2,64,2048]{3,2,1,0:T(8,128)(2,1)} %all-gather.5.cloned.1.call-done.g_ref, bf16[2,896,2048]{2,1,0:T(8,128)(2,1)} %get-tuple-element.9.a_ref, ...), custom_call_target="tpu_custom_call" | custom-call | flops 7516192768 | bytes 41943040 | tf_op jit(solution)/shard_map/raw/pallas_call | solution.py:192
  148.6 1.4 reduce.1
  149.9 4.3 %all-to-all-start.2 = ((f32[8,2,256]{2,1,0:T(2,128)}), f32[8,2,256]{2,1,0:T(2,128)S(1)}, u32[]{:S(2)}, u32[]{:S(2)}) async-start(f32[8,2,256]{2,1,0:T(2,128)} %bitcast.5), calls=%async_computation.2 | async-start | bytes 32768 | tf_op jit(solution)/shard_map/all_to_all | solution.py:231
  154.2 23.0 %back.1 = bf16[16,128,896]{2,1,0:T(8,128)(2,1)} custom-call(s32[16,8,128]{2,1,0:T(8,128)} %bitcast.11, bf16[16,2,64,2048]{3,2,1,0:T(8,128)(2,1)} %all-gather.5.cloned.1.call-done.g_ref, bf16[2,896,2048]{2,1,0:T(8,128)(2,1)} %get-tuple-element.8.q_ref), custom_call_target="tpu_custom_call" | custom-call | flops 7516192768 | bytes 20971520 | tf_op jit(solution)/shard_map/back/pallas_call | solution.py:153
  177.2 0.0 all-to-all-done.2
  177.2 6.5 %all-to-all-start.1 = ((bf16[16,128,896]{2,1,0:T(8,128)(2,1)}), bf16[16,128,896]{2,1,0:T(8,128)(2,1)}, u32[]{:S(2)}, u32[]{:S(2)}) async-start(bf16[16,128,896]{2,1,0:T(8,128)(2,1)} %back.1), calls=%async_computation.1 | async-start | bytes 7340032 | tf_op jit(solution)/shard_map/all_to_all | solution.py:227
  183.8 0.6 broadcast_multiply_fusion
  184.4 55.4 %all-to-all-done.1 = bf16[16,128,896]{2,1,0:T(8,128)(2,1)} async-done(((bf16[16,128,896]{2,1,0:T(8,128)(2,1)}), bf16[16,128,896]{2,1,0:T(8,128)(2,1)}, u32[]{:S(2)}, u32[]{:S(2)}) %all-to-all-start.1) | async-done | bytes 3670048 | tf_op jit(solution)/shard_map/all_to_all | solution.py:227
  239.8 3.3 %reduce_sum.21 = bf16[128,896]{1,0:T(8,128)(2,1)} reduce(bf16[16,128,896]{2,1,0:T(8,128)(2,1)} %all-to-all-done.1, bf16[]{:T(256)} %constant.1.clone.1), dimensions={0}, to_apply=%region_0.0 | reduce | flops 1720320 | bytes 3899394 | tf_op jit(solution)/shard_map/reduce_sum | solution.py:229
  (1 shorter events, 0.0 us)
Async XLA Ops:
  7.2 91.4 %all-gather.7.cloned.1.call-start = ((), (), s32[]{:S(2)}) async-start(), calls=%async_computation.4 | async-start | bytes 3899392 | tf_op jit(solution)/shard_map/all_gather | solution.py:221
  7.9 115.6 %all-gather.5.cloned.1.call-start = ((), (), s32[]{:S(2)}) async-start(), calls=%async_computation.3 | async-start | bytes 9437184 | tf_op jit(solution)/shard_map/all_gather | solution.py:224
  149.9 27.3 %all-to-all-start.2 = ((f32[8,2,256]{2,1,0:T(2,128)}), f32[8,2,256]{2,1,0:T(2,128)S(1)}, u32[]{:S(2)}, u32[]{:S(2)}) async-start(f32[8,2,256]{2,1,0:T(2,128)} %bitcast.5), calls=%async_computation.2 | async-start | bytes 32768 | tf_op jit(solution)/shard_map/all_to_all | solution.py:231
  177.2 62.6 %all-to-all-start.1 = ((bf16[16,128,896]{2,1,0:T(8,128)(2,1)}), bf16[16,128,896]{2,1,0:T(8,128)(2,1)}, u32[]{:S(2)}, u32[]{:S(2)}) async-start(bf16[16,128,896]{2,1,0:T(8,128)(2,1)} %back.1), calls=%async_computation.1 | async-start | bytes 7340032 | tf_op jit(solution)/shard_map/all_to_all | solution.py:227
Sparse Core Ops, SparseCore 0:
  10.1 57.9 all-gather.6
  69.8 53.6 all-gather.4

commit v2 on v1

--- a/solution.py
+++ b/solution.py
@@ -75,39 +75,315 @@
     )(ids_rows, cot)
 
 
-def quant_kernel(w_ref, s_ref, q_ref, a_ref, b_ref):
-    rows, width = w_ref.shape[1:]
-    step_rows, step_cols = 16, 512
-    for col in range(0, width, step_cols):
-        cols = pl.ds(col, step_cols)
-        s = s_ref[0, :, cols]
-        inv7 = 1.0 / (qmax * s)
-
-        def body(k, carry):
-            at = pl.ds(pl.multiple_of(k * step_rows, step_rows), step_rows)
-            w = w_ref[0, at, cols].astype(F32)
-            q, slopes, step_slopes = quantize(w, s, inv7)
-            q_ref[0, at, cols] = q.astype(BF16)
-            a_ref[0, at, cols] = slopes.astype(BF16)
-            b_ref[0, at, cols] = step_slopes.astype(BF16)
-            return carry
-
-        lax.fori_loop(0, rows // step_rows, body, 0, unroll=2)
-
-
-def quant(weights, steps):
+TILE = 128
+STEP_COLS = 512
+STEP_ROWS = 16
+
+
+def ring4(pos, device, view, send, recv):
+    up, down, far = lax.rem(pos + 1, 4), lax.rem(pos + 3, 4), lax.rem(pos + 2, 4)
+
+    def copy(src, k, part, k_to, n):
+        return pltpu.make_async_remote_copy(
+            src_ref=view(k, part) if src is None else src,
+            dst_ref=view(k, part),
+            send_sem=send.at[n],
+            recv_sem=recv.at[n],
+            device_id=device(k_to),
+            device_id_type=pl.DeviceIdType.MESH,
+        )
+
+    class Ring:
+        def start(self, src=None):
+            copy(src, pos, "all", up, 0).start()
+            copy(src, pos, "all", down, 1).start()
+
+        def from_down(self):
+            copy(None, down, "all", up, 0).wait_recv()
+            copy(None, down, "lo", up, 2).start()
+
+        def from_up(self):
+            copy(None, up, "all", down, 1).wait_recv()
+            copy(None, up, "hi", down, 3).start()
+
+        def finish(self):
+            copy(None, far, "lo", up, 2).wait_recv()
+            copy(None, far, "hi", down, 3).wait_recv()
+
+        def drain(self):
+            copy(None, pos, "all", up, 0).wait_send()
+            copy(None, pos, "all", down, 1).wait_send()
+            copy(None, down, "lo", up, 2).wait_send()
+            copy(None, up, "hi", down, 3).wait_send()
+
+    return Ring()
+
+
+def exchange_kernel(
+    packed, tokens, ids, steps, weights,
+    g, x, ids_all, q, slopes, step_slopes,
+    steps_all, w_buf, o_buf,
+    a2a_send, a2a_recv, pair_send, pair_recv, z_send, z_recv, x_send, x_recv,
+    ids_send, ids_recv, steps_send, steps_recv, own_sem, w_sem, o_sem,
+):
+    me, part = lax.axis_index("expert"), lax.axis_index("mp")
+    groups, parts = lax.axis_size("expert"), lax.axis_size("mp")
+    row, col = me // 4, lax.rem(me, 4)
+    z, core = part // 2, lax.rem(part, 2)
+    width = packed.shape[-1]
+
+    def remote(src, dst, send, recv, expert, mp):
+        return pltpu.make_async_remote_copy(
+            src_ref=src, dst_ref=dst, send_sem=send, recv_sem=recv,
+            device_id=(expert, mp), device_id_type=pl.DeviceIdType.MESH,
+        )
+
+    barrier = pltpu.get_barrier_semaphore()
+    for k in range(1, groups):
+        pl.semaphore_signal(barrier, 1, device_id=(lax.rem(me + k, groups), part), device_id_type=pl.DeviceIdType.MESH)
+    for k in range(1, parts):
+        pl.semaphore_signal(barrier, 1, device_id=(me, lax.rem(part + k, parts)), device_id_type=pl.DeviceIdType.MESH)
+    first_w = pltpu.make_async_copy(weights.at[0, pl.ds(0, TILE), :], w_buf.at[0], w_sem.at[0])
+    first_w.start()
+
+    def lanes(p):
+        return pl.ds(pl.multiple_of(p * width, width), width)
+
+    own_g = pltpu.make_async_copy(packed.at[me], g.at[:, me, :, lanes(part)], own_sem.at[0])
+    own_x = pltpu.make_async_copy(tokens, x.at[row, col], own_sem.at[1])
+    own_ids = pltpu.make_async_copy(ids, ids_all.at[me], own_sem.at[2])
+    own_steps = pltpu.make_async_copy(steps, steps_all.at[part], own_sem.at[3])
+    for own in (own_g, own_x, own_ids, own_steps):
+        own.start()
+    pl.semaphore_wait(barrier, groups + parts - 2)
+
+    steps_sent = [
+        remote(steps, steps_all.at[part], steps_send.at[k], steps_recv.at[k], me, lax.rem(part + k, parts))
+        for k in range(1, parts)
+    ]
+    for copy in steps_sent:
+        copy.start()
+
+    def a2a(r, k):
+        to = lax.rem(row - r + 4, 4) * 4 + lax.rem(col + k, 4)
+        return remote(packed.at[to], g.at[:, me, :, lanes(part)], a2a_send.at[r, k], a2a_recv.at[r, k], to, part)
+
+    def a2a_wait(r):
+        for k in range(4):
+            if r or k:
+                source = lax.rem(row + r, 4) * 4 + lax.rem(col - k + 4, 4)
+                remote(packed.at[source], g.at[:, source, :, lanes(part)], a2a_send.at[r, k], a2a_recv.at[r, k], source, part).wait_recv()
+
+    pairs = [(r, k) for r in range(4) for k in range(4) if r or k]
+    for r, k in pairs:
+        a2a(r, k).start()
+
+    ids_sent = [
+        remote(ids, ids_all.at[me], ids_send.at[k], ids_recv.at[k], lax.rem(me + k, groups), part) for k in range(1, groups)
+    ]
+    for copy in ids_sent:
+        copy.start()
+
+    half = tokens.shape[0] // 2
+    quarter = half // 2
+
+    def on_x(k):
+        return (row * 4 + k, part)
+
+    def on_y(k):
+        return (k * 4 + col, part)
+
+    def x_rows(k, piece, base):
+        return pl.ds(base + (quarter if piece == "hi" else 0), half if piece == "all" else quarter)
+
+    def x_pair(piece):
+        return pl.ds(2 if piece == "hi" else 0, 4 if piece == "all" else 2)
+
+    x1a = ring4(col, on_x, lambda k, piece: x.at[row, k, x_rows(k, piece, 0)], x_send.at[0], x_recv.at[0])
+    x1b = ring4(row, on_y, lambda k, piece: x.at[k, col, x_rows(k, piece, half)], x_send.at[1], x_recv.at[1])
+    x2a = ring4(row, on_y, lambda k, piece: x.at[k, x_pair(piece), pl.ds(0, half)], x_send.at[2], x_recv.at[2])
+    x2b = ring4(col, on_x, lambda k, piece: x.at[x_pair(piece), k, pl.ds(half, half)], x_send.at[3], x_recv.at[3])
+    x1a.start(tokens.at[pl.ds(0, half)])
+    x1b.start(tokens.at[pl.ds(half, half)])
+
+    def on_z(k):
+        return (me, k * 2 + core)
+
+    def g_view(r, owner):
+        sources = pl.ds(pl.multiple_of(lax.rem(row + r, 4) * 4, 4), 4)
+
+        def view(k, piece):
+            some = {"all": pl.ds(0, 2), "lo": pl.ds(0, 1), "hi": pl.ds(1, 1)}[piece]
+            return g.at[some, sources, :, lanes(k * 2 + owner)]
+
+        return view
+
+    z_rings = [ring4(z, on_z, g_view(r, core), z_send.at[r], z_recv.at[r]) for r in range(4)]
+
+    def to_pair(r, n):
+        view = g_view(r, core)(lax.rem(z + (0, 3, 1, 2)[n], 4), "all")
+        return remote(view, view, pair_send.at[r, n], pair_recv.at[r, n], me, z * 2 + 1 - core)
+
+    def from_pair(r, n):
+        view = g_view(r, 1 - core)(lax.rem(z + (0, 3, 1, 2)[n], 4), "all")
+        return remote(view, view, pair_send.at[r, n], pair_recv.at[r, n], me, z * 2 + 1 - core)
+
+    def arrive(r):
+        def event():
+            a2a_wait(r)
+            if r == 0:
+                own_g.wait()
+            z_rings[r].start()
+            to_pair(r, 0).start()
+
+        return event
+
+    def down(r):
+        def event():
+            z_rings[r].from_down()
+            to_pair(r, 1).start()
+            z_rings[r].from_up()
+            to_pair(r, 2).start()
+
+        return event
+
+    def far(r):
+        def event():
+            z_rings[r].finish()
+            to_pair(r, 3).start()
+
+        return event
+
+    def x_mid():
+        for ring in (x1a, x1b):
+            ring.from_down()
+            ring.from_up()
+
+    def x_second():
+        own_x.wait()
+        for ring, other in ((x1a, x2a), (x1b, x2b)):
+            ring.finish()
+            other.start()
+
+    def x_mid2():
+        for ring in (x2a, x2b):
+            ring.from_down()
+            ring.from_up()
+
+    tiles_each = weights.shape[1] // TILE
+    tiles = weights.shape[0] * tiles_each
+    outs = (q, slopes, step_slopes)
+
+    def w_in(t, slot):
+        at = pl.ds(pl.multiple_of(lax.rem(t, tiles_each) * TILE, TILE), TILE)
+        return pltpu.make_async_copy(weights.at[t // tiles_each, at, :], w_buf.at[slot], w_sem.at[slot])
+
+    def q_out(t, slot, n):
+        at = pl.ds(pl.multiple_of(lax.rem(t, tiles_each) * TILE, TILE), TILE)
+        return pltpu.make_async_copy(o_buf.at[slot, n], outs[n].at[t // tiles_each, at, :], o_sem.at[slot, n])
+
+    def tile(t, carry):
+        slot = lax.rem(t, 2)
+        w_in(t, slot).wait()
+
+        @pl.when(t + 1 < tiles)
+        def _():
+            w_in(t + 1, 1 - slot).start()
+
+        @pl.when(t >= 2)
+        def _():
+            for n in range(3):
+                q_out(t - 2, slot, n).wait()
+
+        e = t // tiles_each
+
+        def chunk(j, carry):
+            cols = pl.ds(pl.multiple_of(j * STEP_COLS, STEP_COLS), STEP_COLS)
+            per = STEP_COLS // width
+            s = jnp.concatenate([steps_all[j * per + n, pl.ds(e, 1), :] for n in range(per)], axis=1)
+            inv7 = 1.0 / (qmax * s)
+
+            def rows(k, carry):
+                at = pl.ds(pl.multiple_of(k * STEP_ROWS, STEP_ROWS), STEP_ROWS)
+                level, slope, step_slope = quantize(w_buf[slot, at, cols].astype(F32), s, inv7)
+                o_buf[slot, 0, at, cols] = level.astype(BF16)
+                o_buf[slot, 1, at, cols] = slope.astype(BF16)
+                o_buf[slot, 2, at, cols] = step_slope.astype(BF16)
+                return carry
+
+            return lax.fori_loop(0, TILE // STEP_ROWS, rows, carry, unroll=2)
+
+        lax.fori_loop(0, weights.shape[2] // STEP_COLS, chunk, 0)
+        for n in range(3):
+            q_out(t, slot, n).start()
+        return carry
+
+    own_steps.wait()
+    for copy in steps_sent:
+        copy.wait_recv()
+
+    plan = (
+        (1, arrive(0)), (3, arrive(1)), (5, arrive(2)), (6, down(0)), (7, arrive(3)), (8, x_mid), (9, down(1)),
+        (10, x_second), (11, far(0)), (12, down(2)), (13, x_mid2), (14, far(1)), (14, down(3)), (14, far(2)), (14, far(3)),
+    )
+    done = 0
+    for until, event in plan:
+        if until > done:
+            lax.fori_loop(done, until, tile, 0)
+            done = until
+        event()
+
+    for t in (tiles - 2, tiles - 1):
+        for n in range(3):
+            q_out(t, t % 2, n).wait()
+    for ring in (x2a, x2b):
+        ring.finish()
+    own_ids.wait()
+    for copy in ids_sent:
+        copy.wait_recv()
+    for r in range(4):
+        for n in range(4):
+            from_pair(r, n).wait_recv()
+    for copy in steps_sent + ids_sent:
+        copy.wait_send()
+    for r, k in pairs:
+        a2a(r, k).wait_send()
+    for ring in (x1a, x1b, x2a, x2b, *z_rings):
+        ring.drain()
+    for r in range(4):
+        for n in range(4):
+            to_pair(r, n).wait_send()
+
+
+def exchange(packed, tokens, ids, steps, weights):
+    groups, local, cap, part_f = packed.shape
+    parts = lax.axis_size("mp")
     e, d, f = weights.shape
-    tile = 128
-    block = pl.BlockSpec((1, tile, f), lambda i, j: (i, j, 0))
+    toks, width = tokens.shape
+    dma = pltpu.SemaphoreType.DMA
+    vmem = pl.BlockSpec(memory_space=pltpu.VMEM)
+    anywhere = pl.BlockSpec(memory_space=pl.ANY)
     return pl.pallas_call(
-        quant_kernel,
-        grid=(e, d // tile),
-        in_specs=[block, pl.BlockSpec((1, 1, f), lambda i, j: (i, 0, 0))],
-        out_specs=[block] * 3,
-        out_shape=[jax.ShapeDtypeStruct((e, d, f), BF16)] * 3,
-        cost_estimate=pl.CostEstimate(flops=50 * e * d * f, bytes_accessed=8 * e * d * f, transcendentals=e * d * f),
-        name="quant",
-    )(weights, steps)
+        exchange_kernel,
+        in_specs=[vmem] * 4 + [anywhere],
+        out_specs=[anywhere] * 6,
+        out_shape=[
+            jax.ShapeDtypeStruct((local, groups, cap, f), BF16),
+            jax.ShapeDtypeStruct((4, groups // 4, toks, width), BF16),
+            jax.ShapeDtypeStruct((groups, *ids.shape), jnp.int32),
+            *[jax.ShapeDtypeStruct((e, d, f), BF16)] * 3,
+        ],
+        scratch_shapes=[
+            pltpu.VMEM((parts, *steps.shape), F32),
+            pltpu.VMEM((2, TILE, f), BF16),
+            pltpu.VMEM((2, 3, TILE, f), BF16),
+            dma((4, 4)), dma((4, 4)), dma((4, 4)), dma((4, 4)), dma((4, 4)), dma((4, 4)), dma((4, 4)), dma((4, 4)),
+            dma((groups,)), dma((groups,)), dma((parts,)), dma((parts,)), dma((4,)), dma((2,)), dma((2, 3)),
+        ],
+        compiler_params=pltpu.CompilerParams(collective_id=0, has_side_effects=True),
+        cost_estimate=pl.CostEstimate(flops=50 * e * d * f, bytes_accessed=60 << 20, transcendentals=e * d * f),
+        name="exchange",
+    )(packed, tokens, ids, steps, weights)
 
 
 def selection(ids_ref, first, local, cap):
@@ -147,7 +423,7 @@
 
 
 def back(ids, g, q):
-    groups, local, cap, f = g.shape
+    local, groups, cap, f = g.shape
     d = q.shape[1]
     toks = ids.shape[2]
     return pl.pallas_call(
@@ -155,7 +431,7 @@
         grid=(local,),
         in_specs=[
             pl.BlockSpec(ids.shape, lambda e: (0, 0, 0)),
-            pl.BlockSpec((groups, 1, cap, f), lambda e: (0, e, 0, 0)),
+            pl.BlockSpec((1, groups, cap, f), lambda e: (e, 0, 0, 0)),
             pl.BlockSpec((1, d, f), lambda e: (e, 0, 0)),
         ],
         out_specs=pl.BlockSpec((groups, toks, d), lambda e: (0, 0, 0)),
@@ -185,7 +461,7 @@
 
 
 def raw_grads(ids, x, g, slopes, step_slopes):
-    groups, local, cap, f = g.shape
+    local, groups, cap, f = g.shape
     d = slopes.shape[1]
     tile = 256
     block = pl.BlockSpec((1, d, tile), lambda e, j: (e, 0, j))
@@ -195,7 +471,7 @@
         in_specs=[
             pl.BlockSpec(ids.shape, lambda e, j: (0, 0, 0)),
             pl.BlockSpec(x.shape, lambda e, j: (0, 0, 0)),
-            pl.BlockSpec((groups, 1, cap, tile), lambda e, j: (0, e, 0, j)),
+            pl.BlockSpec((1, groups, cap, tile), lambda e, j: (e, 0, 0, j)),
             block,
             block,
         ],
@@ -217,12 +493,9 @@
     width = tokens.shape[1]
     part_f = cotangent.shape[2]
     packed = pack(expert_ids.reshape(-1, 128), cotangent.reshape(toks * top_k, part_f), cap, experts)
-    ids = lax.all_gather(expert_ids.T, "expert", axis=0)
-    x = lax.all_gather(tokens, "expert", axis=0)
-    full_steps = lax.all_gather(steps, "mp", axis=1, tiled=True).reshape(local, 1, -1)
-    g_part = lax.all_to_all(packed.reshape(groups, local, cap, part_f), "expert", split_axis=0, concat_axis=0, tiled=True)
-    g = lax.all_gather(g_part, "mp", axis=3, tiled=True)
-    q, slopes, step_slopes = quant(weights, full_steps)
+    packed = packed.reshape(groups, local, cap, part_f)
+    g, x, ids, q, slopes, step_slopes = exchange(packed, tokens, expert_ids.T, steps, weights)
+    x = x.reshape(groups, toks, width)
     backs = back(ids, g, q)
     returned = lax.all_to_all(backs, "expert", split_axis=0, concat_axis=0, tiled=True)
     weight_out, partial_steps = raw_grads(ids, x, g, slopes, step_slopes)

time: 251 us -> 181 us (0.72)
  blocking collectives: 61 us -> 0 us
  Pallas kernels: 75.5 us -> 109 us
  waiting for transfers between devices: 81.1 us -> 55.4 us
  between operations: 14.1 us -> 0.66 us
  starting transfers between devices: 10.9 us -> 8.12 us
    all_gather x2 -> x0, blocking collectives: 34.2 us -> none  [the longest x1 18.8 us: per_device(): ids = lax.all_gather(expert_ids.T, 'expert', axis=0)]
    pallas_call x1, Pallas kernels: 24.1 us -> 57.9 us  [exchange(): pl.pallas_call(exchange_kernel, in_specs=[vmem] * 4 + [anywhere], out_spe...]
    all_to_all x1 -> x0, blocking collectives: 26.8 us -> none  [per_device(): lax.all_to_all(packed.reshape(groups, local, cap, part_f), 'expert', spli...]
    all_gather x2 -> x0, waiting for transfers between devices: 25 us -> none  [the longest x1 25 us: per_device(): g = lax.all_gather(g_part, 'mp', axis=3, tiled=True)]
  transfers between devices with their start and end apart: 4 -> 2, of which waited for: 2 -> 1; matrix products, arithmetic and copies ran while one was open for 1% -> 0% of each run, Pallas kernels for 20% -> 13%
where the time goes in v2:
time: 181 us; the launch traced here: 180 us
  Pallas kernels  109 us (60%)
  waiting for transfers between devices  55.4 us (31%)
  starting transfers between devices  8.12 us (4%)
  other arithmetic  5.26 us (3%)
    pallas_call x1, Pallas kernels, exchange(): pl.pallas_call(exchange_kernel, in_specs=[vmem] * 4 + [anywhere], out_spe...  57.9 us
    all_to_all x1, waiting for transfers between devices, per_device(): lax.all_to_all(backs, 'expert', split_axis=0, concat_axis=0, tiled=True)  55.4 us
    pallas_call x1, Pallas kernels, raw_grads(): pl.pallas_call(functools.partial(raw_kernel, cap), grid=(local, f // tile...  25.2 us
    pallas_call x1, Pallas kernels, back(): pl.pallas_call(functools.partial(back_kernel, cap), grid=(local,), in_spe...  23 us
    all_to_all x1, starting transfers between devices, per_device(): lax.all_to_all(backs, 'expert', split_axis=0, concat_axis=0, tiled=True)  4.65 us
  transfers between devices with their start and end apart: 2, of which 1 were waited for; matrix products, arithmetic and copies ran while one was open for 0% of the time, Pallas kernels for 13%

profile of v2, /device:TPU:1, one launch (start us, length us, event | category | flops | bytes accessed | tf_op | source)
XLA Modules:
  0.0 180.3 jit_solution(3514179747605152819)
XLA Ops:
  0.6 0.8 copy.10
  1.4 0.7 reshape.21.ids_ref
  2.1 3.4 %pack.1 = bf16[2048,256]{1,0:T(8,128)(2,1)} custom-call(s32[8,128]{1,0:T(8,128)} %reshape.21.ids_ref, bf16[1024,256]{1,0:T(8,128)(2,1)} %bitcast.8), custom_call_target="tpu_custom_call" | custom-call | tf_op jit(solution)/shard_map/pack/pallas_call | solution.py:71
  5.5 57.9 %exchange.1 = (bf16[2,16,64,2048]{3,2,1,0:T(8,128)(2,1)}, bf16[4,4,128,896]{3,2,1,0:T(8,128)(2,1)}, s32[16,8,128]{2,1,0:T(8,128)}, bf16[2,896,2048]{2,1,0:T(8,12...) custom-call(bf16[16,2,64,256]{3,2,1,0:T(8,128)(2,1)} %bitcast.7, bf16[128,896]{1,0:T(8,128)(2,1)} %tokens.1, ...), custom_call_target="tpu_custom_call" | custom-call | flops 183500800 | bytes 62914560 | tf_op jit(solution)/shard_map/exchange/pallas_call | solution.py:366
  63.4 25.2 %raw.1 = (bf16[2,896,2048]{2,1,0:T(8,128)(2,1)}, f32[2,1,2048]{2,1,0:T(1,128)}) custom-call(s32[16,8,128]{2,1,0:T(8,128)} %get-tuple-element.11.ids_ref, bf16[16,128,896]{2,1,0:T(8,128)(2,1)} %bitcast.10, bf16[2,16,64,2048]{3,2,1,0:T(8,128)(2,1)} %get-tuple-element.12.g_ref, bf16[2,896,2048]{2,1,0:T(8,128)(2,1)} %get-tuple-element.15.a_ref, ...), custom_call_target="tpu_custom_call" | custom-call | flops 7516192768 | bytes 41943040 | tf_op jit(solution)/shard_map/raw/pallas_call | solution.py:468
  88.6 1.4 reduce.1
  90.0 3.5 %all-to-all-start.1 = ((f32[8,2,256]{2,1,0:T(2,128)}), f32[8,2,256]{2,1,0:T(2,128)S(1)}, u32[]{:S(2)}, u32[]{:S(2)}) async-start(f32[8,2,256]{2,1,0:T(2,128)} %bitcast.4), calls=%async_computation.1 | async-start | bytes 32768 | tf_op jit(solution)/shard_map/all_to_all | solution.py:504
  93.4 23.0 %back.1 = bf16[16,128,896]{2,1,0:T(8,128)(2,1)} custom-call(s32[16,8,128]{2,1,0:T(8,128)} %get-tuple-element.11.ids_ref, bf16[2,16,64,2048]{3,2,1,0:T(8,128)(2,1)} %get-tuple-element.12.g_ref, bf16[2,896,2048]{2,1,0:T(8,128)(2,1)} %get-tuple-element.13.q_ref), custom_call_target="tpu_custom_call" | custom-call | flops 7516192768 | bytes 20971520 | tf_op jit(solution)/shard_map/back/pallas_call | solution.py:429
  116.4 0.0 all-to-all-done.1
  116.4 4.7 %all-to-all-start = ((bf16[16,128,896]{2,1,0:T(8,128)(2,1)}), bf16[16,128,896]{2,1,0:T(8,128)(2,1)}, u32[]{:S(2)}, u32[]{:S(2)}) async-start(bf16[16,128,896]{2,1,0:T(8,128)(2,1)} %back.1), calls=%async_computation | async-start | bytes 7340032 | tf_op jit(solution)/shard_map/all_to_all | solution.py:500
  121.1 0.6 broadcast_multiply_fusion
  121.7 55.4 %all-to-all-done = bf16[16,128,896]{2,1,0:T(8,128)(2,1)} async-done(((bf16[16,128,896]{2,1,0:T(8,128)(2,1)}), bf16[16,128,896]{2,1,0:T(8,128)(2,1)}, u32[]{:S(2)}, u32[]{:S(2)}) %all-to-all-start) | async-done | bytes 3670048 | tf_op jit(solution)/shard_map/all_to_all | solution.py:500
  177.0 3.3 %reduce_sum.21 = bf16[128,896]{1,0:T(8,128)(2,1)} reduce(bf16[16,128,896]{2,1,0:T(8,128)(2,1)} %all-to-all-done, bf16[]{:T(256)} %constant.1.clone.1), dimensions={0}, to_apply=%region_0.0 | reduce | flops 1720320 | bytes 3899394 | tf_op jit(solution)/shard_map/reduce_sum | solution.py:502
  (1 shorter events, 0.0 us)
Async XLA Ops:
  90.0 26.5 %all-to-all-start.1 = ((f32[8,2,256]{2,1,0:T(2,128)}), f32[8,2,256]{2,1,0:T(2,128)S(1)}, u32[]{:S(2)}, u32[]{:S(2)}) async-start(f32[8,2,256]{2,1,0:T(2,128)} %bitcast.4), calls=%async_computation.1 | async-start | bytes 32768 | tf_op jit(solution)/shard_map/all_to_all | solution.py:504
  116.4 60.6 %all-to-all-start = ((bf16[16,128,896]{2,1,0:T(8,128)(2,1)}), bf16[16,128,896]{2,1,0:T(8,128)(2,1)}, u32[]{:S(2)}, u32[]{:S(2)}) async-start(bf16[16,128,896]{2,1,0:T(8,128)(2,1)} %back.1), calls=%async_computation | async-start | bytes 7340032 | tf_op jit(solution)/shard_map/all_to_all | solution.py:500
